TPU v7x, 8 devices: a whole 2x2x1 slice. The times are simulated.
8 devices in a mesh: dp: 2 (over y, z), ep: 4 (over x, core).
Axes of the slice: x: 2, y: 2, z: 1, core: 2. Of those that a mesh axis runs over, the one named last changes fastest.
Arguments:
- x: bfloat16 [2, 4, 256, 3584], P('dp', 'ep'), parts along dimension 0
- expert: int32 [2, 4, 256, 8], P('dp', 'ep'), parts along dimension 0
- slot: int32 [2, 4, 256, 8], P('dp', 'ep'), parts along dimension 0
- gate: float32 [2, 4, 256, 8], P('dp', 'ep'), parts along dimension 0
- w_gate: bfloat16 [32, 3584, 2560], P('ep')
- w_up: bfloat16 [32, 3584, 2560], P('ep')
- w_down: bfloat16 [32, 2560, 3584], P('ep')
- s_gate: bfloat16 [3584, 20480], replicated
- s_up: bfloat16 [3584, 20480], replicated
- s_down: bfloat16 [20480, 3584], replicated
Outputs:
- y: bfloat16 [2, 4, 256, 3584], P('dp', 'ep'), parts along dimension 0
There are 2 independent parts. A program takes and returns all parts, laid end to end along the dimension named above; an argument that names none is the same for every part.
All inputs are finite; a program needn't handle non-finite values.
Results may differ from a plain program's by a relative error of at most 0.009.
Values are sent between devices in bfloat16 or wider.
A program may use at most 2.25 GiB of HBM per device.

v0:
```python
import jax
import jax.numpy as jnp
from jax import lax
from jax.experimental import pallas as pl
from jax.experimental.pallas import tpu as pltpu
from jax.sharding import PartitionSpec as P

CHUNK = 16
VMEM_LIMIT = 66_500_000
X, Y, CORE = 2, 4, 1


def dot(a, b):
    return jnp.dot(a, b, preferred_element_type=jnp.float32)


def swiglu(g, u):
    return (g * jax.nn.sigmoid(g) * u).astype(jnp.bfloat16)


def params(n):
    return pltpu.CompilerParams(
        vmem_limit_bytes=VMEM_LIMIT, dimension_semantics=("arbitrary",) * n
    )


def place():
    ep = lax.axis_index("ep")
    return lax.axis_index("dp"), ep // 2, ep % 2


def peer(bits):
    y, x, core = place()
    y = 1 - y if bits & Y else y
    x = 1 - x if bits & X else x
    core = 1 - core if bits & CORE else core
    return (y, x * 2 + core)


def gather_up(x, small, sg, su, per_core, blocks, relay, bf):
    tokens, d = x.shape
    half = tokens // 2

    def kern(x_ref, small_ref, g_ref, u_ref, h_ref, all_x, all_small, x2, local, send, recv):
        i = pl.program_id(0)

        def copy(n, src, dst, bits):
            return pltpu.make_async_remote_copy(
                src_ref=src,
                dst_ref=dst,
                send_sem=send.at[n],
                recv_sem=recv.at[n],
                device_id=peer(bits),
                device_id_type=pl.DeviceIdType.MESH,
            )

        def at(bits):
            return all_x.at[bits - 1]

        top, bottom = pl.ds(0, half), pl.ds(half, half)
        first = [copy(n, x_ref, at(b), b) for n, b in enumerate((CORE, X, Y))]
        second = [
            copy(3, at(Y).at[top], at(X | Y).at[top], X),
            copy(4, at(X).at[bottom], at(X | Y).at[bottom], Y),
            copy(5, at(X), at(X | CORE), CORE),
            copy(6, at(Y), at(Y | CORE), CORE),
        ]
        third = [copy(7, at(X | Y), at(X | Y | CORE), CORE)]
        little = [copy(7 + b, small_ref, all_small.at[b - 1], b) for b in range(1, 8)]

        def up(v):
            return swiglu(dot(v, g_ref[...]), dot(v, u_ref[...]))

        @pl.when(i == 0)
        def _():
            own = pltpu.make_async_copy(x_ref, x2.at[pl.ds(0, tokens)], local.at[0])
            own.start()
            barrier = pltpu.get_barrier_semaphore()
            for bits in range(1, 8):
                pl.semaphore_signal(
                    barrier, inc=1, device_id=peer(bits), device_id_type=pl.DeviceIdType.MESH
                )
            pl.semaphore_wait(barrier, 7)
            for c in little + first:
                c.start()
            own.wait()
            h_ref[:tokens] = up(x2[:tokens])
            first[0].wait_recv()
            other = pltpu.make_async_copy(at(CORE), x2.at[pl.ds(tokens, tokens)], local.at[1])
            other.start()
            other.wait()
            h_ref[tokens:] = up(x2[tokens:])

        @pl.when(i == relay)
        def _():
            first[1].wait_recv()
            first[2].wait_recv()
            for c in second:
                c.start()

        @pl.when(i > 0)
        def _():
            h_ref[...] = up(x2[...])

        @pl.when(i == blocks - 1)
        def _():
            second[0].wait_recv()
            second[1].wait_recv()
            third[0].start()
            second[2].wait_recv()
            second[3].wait_recv()
            for c in little:
                c.wait_recv()
            third[0].wait_recv()
            for c in first + second + third + little:
                c.wait_send()

    def column(i):
        return (0, (lax.axis_index("ep") % 2) * per_core + i)

    any_spec = pl.BlockSpec(memory_space=pl.ANY)
    return pl.pallas_call(
        kern,
        out_shape=[
            jax.ShapeDtypeStruct((2 * tokens, blocks * bf), jnp.bfloat16),
            jax.ShapeDtypeStruct((7, tokens, d), x.dtype),
            jax.ShapeDtypeStruct((7, *small.shape), small.dtype),
        ],
        grid=(blocks,),
        in_specs=[any_spec] * 2 + [pl.BlockSpec((d, bf), column)] * 2,
        out_specs=[pl.BlockSpec((2 * tokens, bf), lambda i: (0, i)), any_spec, any_spec],
        scratch_shapes=[
            pltpu.VMEM((2 * tokens, d), jnp.bfloat16),
            pltpu.SemaphoreType.DMA((2,)),
            pltpu.SemaphoreType.DMA((15,)),
            pltpu.SemaphoreType.DMA((15,)),
        ],
        compiler_params=pltpu.CompilerParams(
            vmem_limit_bytes=VMEM_LIMIT,
            dimension_semantics=("arbitrary",),
            collective_id=0,
            has_side_effects=True,
        ),
        cost_estimate=pl.CostEstimate(
            flops=8 * tokens * d * bf * blocks,
            bytes_accessed=4 * d * bf * blocks,
            transcendentals=2 * tokens * bf * blocks,
        ),
        name="gather_up",
    )(x, small, sg, su)


def reduce_up_down(x, xs, h, out, codes, gates, sg, su, sd, slots, bf):
    half, d = x.shape
    mid = half // 2
    experts, _, chunks = out.shape[:3]
    rows = experts * slots
    top = codes.shape[1]
    m, early = 2 * half, h.shape[1] // bf
    blocks = sd.shape[0] // 2 // bf
    late = blocks - early
    bu = bf // 2
    ups = 2 * late
    order = (7, 5, 3, 6, 1, 0)
    up0 = len(order)
    mid0 = up0 + ups
    down0 = mid0 + 2
    steps = down0 + blocks
    bn = 512
    f32, bf16 = jnp.float32, jnp.bfloat16

    def kern(*refs):
        code_ref, gate_ref, x_ref, xs_ref, out_ref, g_ref, u_ref, h_ref, d_ref, y_ref = refs[:10]
        x2, hs, acc, weight, sends, cores, links, t_ref, b_ref, local, send, recv = refs[10:]
        i = pl.program_id(0)
        top_half, bottom = pl.ds(0, mid), pl.ds(mid, mid)
        own, other = pl.ds(0, half), pl.ds(half, half)
        moves = [
            (sends.at[0], cores.at[0], CORE),
            (sends.at[1], cores.at[1], CORE),
            (x2.at[other], cores.at[2], CORE),
            (sends.at[0].at[top_half], t_ref, Y),
            (sends.at[0].at[bottom], b_ref, X),
            (x2.at[own], links.at[0], X),
            (x2.at[other], links.at[1], Y),
            (sends.at[0], cores.at[3], CORE),
        ]
        copies = [
            pltpu.make_async_remote_copy(
                src_ref=src,
                dst_ref=dst,
                send_sem=send.at[n],
                recv_sem=recv.at[n],
                device_id=peer(bits),
                device_id_type=pl.DeviceIdType.MESH,
            )
            for n, (src, dst, bits) in enumerate(moves)
        ]
        loads = [
            pltpu.make_async_copy(x_ref, x2.at[own], local.at[0]),
            pltpu.make_async_copy(xs_ref.at[CORE - 1], x2.at[other], local.at[1]),
        ]

        def combine(s, put):
            row = lax.broadcasted_iota(jnp.int32, (rows, half), 0).astype(f32)
            w = jnp.zeros(row.shape, f32)
            for j in range(top):
                w = jnp.where(row == code_ref[s, j : j + 1, :], gate_ref[s, j : j + 1, :], w)
            weight[...] = w.T.astype(bf16)

            @pl.loop(0, d // bn)
            def _(n):
                cols = pl.ds(pl.multiple_of(n * bn, bn), bn)
                put(cols, dot(weight[...], out_ref[:, 0, :, 0, :, cols].reshape(rows, bn)))

        @pl.when(i == 0)
        def _():
            barrier = pltpu.get_barrier_semaphore()
            for bits in (CORE, X, Y):
                pl.semaphore_signal(
                    barrier, inc=1, device_id=peer(bits), device_id_type=pl.DeviceIdType.MESH
                )

        for n in range(3):

            @pl.when(i == n)
            def _(n=n):
                def put(cols, y):
                    if n < 2:
                        sends[n, :, cols] = y.astype(bf16)
                    else:
                        x2[other, cols] = y.astype(bf16)

                combine(order[n], put)
                if n == 0:
                    pl.semaphore_wait(pltpu.get_barrier_semaphore(), 3)
                copies[n].start()

        @pl.when(i == 3)
        def _():
            copies[0].wait_send()
            copies[0].wait_recv()

            def put(cols, y):
                sends[0, :, cols] = (y + cores[0, :, cols].astype(f32)).astype(bf16)

            combine(order[3], put)
            copies[3].start()
            copies[4].start()

        for n, where in ((4, other), (5, own)):

            @pl.when(i == n)
            def _(n=n, where=where):
                def put(cols, y):
                    acc[where, cols] = y

                if n == 5:
                    copies[2].wait_send()
                    for c in loads:
                        c.start()
                combine(order[n], put)
                if n == 5:
                    for c in loads:
                        c.wait()

        @pl.when((i >= up0) & (i < mid0))
        def _():
            hs[i - up0] = swiglu(dot(x2[...], g_ref[...]), dot(x2[...], u_ref[...]))

        @pl.when(i == mid0)
        def _():
            copies[2].wait_recv()
            copies[3].wait_recv()

            def put(cols, y):
                y = y + cores[2, :, cols].astype(f32)
                x2[top_half, cols] = (y[:mid] + t_ref[:, cols].astype(f32)).astype(bf16)
                x2[bottom, cols] = y[mid:].astype(bf16)

            combine(2, put)
            copies[5].start()

        @pl.when(i == mid0 + 1)
        def _():
            copies[1].wait_send()
            copies[1].wait_recv()
            copies[4].wait_recv()

            def put(cols, y):
                y = y + cores[1, :, cols].astype(f32)
                x2[pl.ds(half, mid), cols] = y[:mid].astype(bf16)
                x2[pl.ds(half + mid, mid), cols] = (
                    y[mid:] + b_ref[:, cols].astype(f32)
                ).astype(bf16)

            combine(4, put)
            copies[6].start()

        @pl.when((i >= down0) & (i < down0 + late))
        def _():
            j = 2 * (i - down0)
            acc[...] += dot(hs[j], d_ref[:bu]) + dot(hs[j + 1], d_ref[bu:])

        @pl.when(i >= down0 + late)
        def _():
            acc[...] += dot(h_ref[...], d_ref[...])

        @pl.when(i == steps - 1)
        def _():
            copies[3].wait_send()
            copies[4].wait_send()
            sends[0] = acc[other].astype(bf16)
            copies[7].start()
            copies[5].wait_recv()
            copies[6].wait_recv()
            acc[own] += links[0].astype(f32) + links[1].astype(f32)
            copies[7].wait_recv()
            sends[1] = (acc[own] + cores[3].astype(f32)).astype(bf16)
            result = pltpu.make_async_copy(sends.at[1], y_ref, local.at[0])
            result.start()
            for n in (5, 6, 7):
                copies[n].wait_send()
            result.wait()

    def core():
        return lax.axis_index("ep") % 2

    def source(i):
        s = jnp.where(i <= mid0, 2, 4)
        for n, v in enumerate(order):
            s = jnp.where(i == n, v, s)
        return (0, s // 4, 0, s % 4, 0, 0)

    def column(i):
        return (0, 2 * (core() * blocks + early) + jnp.clip(i - up0, 0, ups - 1))

    def down_row(i):
        j = jnp.maximum(i - down0, 0)
        return (core() * blocks + jnp.where(j < late, early + j, j - late), 0)

    any_spec = pl.BlockSpec(memory_space=pl.ANY)
    small_spec = pl.BlockSpec(codes.shape, lambda i: (0, 0, 0))
    dma = pltpu.SemaphoreType.DMA
    return pl.pallas_call(
        kern,
        out_shape=jax.ShapeDtypeStruct((half, d), bf16),
        grid=(steps,),
        in_specs=[small_spec, small_spec, any_spec, any_spec]
        + [pl.BlockSpec((experts, 1, chunks, 1, CHUNK, d), source)]
        + [pl.BlockSpec((d, bu), column)] * 2
        + [
            pl.BlockSpec((m, bf), lambda i: (0, jnp.maximum(i - down0 - late, 0))),
            pl.BlockSpec((bf, d), down_row),
        ],
        out_specs=any_spec,
        scratch_shapes=[
            pltpu.VMEM((m, d), bf16),
            pltpu.VMEM((ups, m, bu), bf16),
            pltpu.VMEM((m, d), f32),
            pltpu.VMEM((half, rows), bf16),
            pltpu.VMEM((2, half, d), bf16),
            pltpu.VMEM((4, half, d), bf16),
            pltpu.VMEM((2, half, d), bf16),
            pltpu.VMEM((mid, d), bf16),
            pltpu.VMEM((mid, d), bf16),
            dma((2,)),
            dma((8,)),
            dma((8,)),
        ],
        compiler_params=pltpu.CompilerParams(
            vmem_limit_bytes=VMEM_LIMIT,
            dimension_semantics=("arbitrary",),
            collective_id=1,
            has_side_effects=True,
        ),
        cost_estimate=pl.CostEstimate(
            flops=2 * m * d * bf * (blocks + 2 * late),
            bytes_accessed=2 * d * bf * (blocks + 2 * late),
            transcendentals=m * bf * late,
        ),
        name="reduce_up_down",
    )(codes, gates, x, xs, out, sg, su, h, sd)


def plan_call(smalls, base, part, slots):
    n_src, _, top, tokens = smalls.shape
    groups = n_src // 4
    experts = 4 * groups

    def kern(base_ref, part_ref, small_ref, code_ref, expert_ref, used_ref):
        low = base_ref[0].astype(jnp.float32)
        codes = [small_ref[s, 0] - low for s in range(n_src)]
        used, total = [], []
        for e in range(experts):
            counts = []
            for grp in range(groups):
                most = jnp.full((top, tokens), -1.0, jnp.float32)
                for s in range(grp * 4, grp * 4 + 4):
                    here = (codes[s] >= e * slots) & (codes[s] < (e + 1) * slots)
                    most = jnp.maximum(most, jnp.where(here, codes[s] - e * slots, -1.0))
                counts.append((jnp.max(most).astype(jnp.int32) + CHUNK) // CHUNK)
            used.append(counts)
            total.append(sum(counts))
        news = [jnp.full((top, tokens), -1.0, jnp.float32) for _ in range(n_src)]
        for e in range(experts):
            rank = jnp.int32(0)
            for o in range(experts):
                if o != e:
                    ahead = total[o] >= total[e] if o < e else total[o] > total[e]
                    rank = rank + ahead.astype(jnp.int32)
            spot = rank // 2
            mine = (rank % 2 + spot % 2) % 2 == part_ref[0]

            @pl.when(mine)
            def _(e=e, spot=spot):
                expert_ref[spot] = e
                for grp in range(groups):
                    used_ref[spot, grp] = used[e][grp]

            shift = jnp.where(mine, (spot - e) * slots, -(10**6)).astype(jnp.float32)
            for s in range(n_src):
                here = (codes[s] >= e * slots) & (codes[s] < (e + 1) * slots)
                news[s] = jnp.where(here, codes[s] + shift, news[s])
        for s in range(n_src):
            code_ref[s] = news[s]

    smem = pl.BlockSpec(memory_space=pltpu.SMEM)
    return pl.pallas_call(
        kern,
        out_shape=[
            jax.ShapeDtypeStruct((n_src, top, tokens), jnp.float32),
            jax.ShapeDtypeStruct((experts // groups,), jnp.int32),
            jax.ShapeDtypeStruct((experts // groups, groups), jnp.int32),
        ],
        in_specs=[smem, smem, pl.BlockSpec(memory_space=pltpu.VMEM)],
        out_specs=[pl.BlockSpec(memory_space=pltpu.VMEM), smem, smem],
        name="plan",
    )(base, part, smalls)


def routed_call(x, xs, codes, picked, used, wg, wu, wd, slots, bf):
    n_src = 1 + xs.shape[0]
    groups = n_src // 4
    experts = picked.shape[0]
    d = x.shape[1]
    ff = wg.shape[2]
    nf = ff // bf
    chunks = slots // CHUNK
    top, tokens = codes.shape[1:]
    rows = 4 * CHUNK
    whole = 6

    def kern(picked_ref, used_ref, code_ref, x_ref, xs_ref, g_ref, u_ref, d_ref, out_ref, z, acc):
        e, f = pl.program_id(0), pl.program_id(1)
        lead = used_ref[e, 0]
        total = lead + used_ref[e, 1]

        @pl.when((e == 0) & (f == 0))
        def _():
            acc[...] = jnp.zeros_like(acc)

        @pl.when(f == 0)
        def _():
            low = (e * slots).astype(jnp.float32)
            row = low + lax.broadcasted_iota(jnp.int32, (slots, tokens), 0).astype(jnp.float32)
            for grp in range(groups):
                for k in range(4):
                    s = grp * 4 + k
                    pick = jnp.zeros((slots, tokens), jnp.float32)
                    for j in range(top):
                        pick = jnp.where(row == code_ref[s, j : j + 1, :], 1.0, pick)
                    pick = pick.astype(jnp.bfloat16)
                    zs = dot(pick, x_ref[...] if s == 0 else xs_ref[s - 1])
                    zs = zs.astype(jnp.bfloat16).reshape(chunks, CHUNK, d)
                    z[pl.ds(0 if grp == 0 else lead, chunks), k] = zs

        def part(first, n):
            m = n * rows
            zz = z[pl.ds(first, n)].reshape(m, d)
            h = swiglu(dot(zz, g_ref[0]), dot(zz, u_ref[0]))
            old = jnp.where(f == 0, 0.0, acc[pl.ds(first, n)].reshape(m, d))
            acc[pl.ds(first, n)] = (old + dot(h, d_ref[0])).reshape(n, rows, d)

        two = total > whole
        head = jnp.where(two, (total + 1) // 2, total)

        def step(i, _):
            n = jnp.where(i == 0, head, total - head)
            for v in range(1, whole + 1):
                pl.when(n == v)(lambda v=v: part(i * head, v))
            return 0

        lax.fori_loop(0, jnp.where(two, 2, 1), step, 0)

        @pl.when(f == nf - 1)
        def _():
            for grp in range(groups):
                o = acc[pl.ds(0 if grp == 0 else lead, chunks)]
                out_ref[0, grp] = o.astype(jnp.bfloat16).reshape(chunks, 4, CHUNK, d)

    total = experts * groups * chunks * rows
    return pl.pallas_call(
        kern,
        out_shape=jax.ShapeDtypeStruct((experts, groups, chunks, 4, CHUNK, d), jnp.bfloat16),
        grid_spec=pltpu.PrefetchScalarGridSpec(
            num_scalar_prefetch=2,
            grid=(experts, nf),
            in_specs=[
                pl.BlockSpec(codes.shape, lambda e, f, p, u: (0, 0, 0)),
                pl.BlockSpec(x.shape, lambda e, f, p, u: (0, 0), pipeline_mode=pl.Buffered(1)),
                pl.BlockSpec(
                    xs.shape, lambda e, f, p, u: (0, 0, 0), pipeline_mode=pl.Buffered(1)
                ),
                pl.BlockSpec((1, d, bf), lambda e, f, p, u: (p[e], 0, f)),
                pl.BlockSpec((1, d, bf), lambda e, f, p, u: (p[e], 0, f)),
                pl.BlockSpec((1, bf, d), lambda e, f, p, u: (p[e], f, 0)),
            ],
            out_specs=pl.BlockSpec(
                (1, groups, chunks, 4, CHUNK, d), lambda e, f, p, u: (e, 0, 0, 0, 0, 0)
            ),
            scratch_shapes=[
                pltpu.VMEM((groups * chunks, 4, CHUNK, d), jnp.bfloat16),
                pltpu.VMEM((groups * chunks, rows, d), jnp.float32),
            ],
        ),
        compiler_params=params(2),
        cost_estimate=pl.CostEstimate(
            flops=4 * total * d * ff,
            bytes_accessed=6 * experts * d * ff,
            transcendentals=total * ff,
        ),
        name="routed",
    )(picked, used, codes, x, xs, wg, wu, wd)


def solution(mesh):
    def body(x, expert, slot, gate, wg, wu, wd, sg, su, sd):
        x = x[0, 0]
        tokens = x.shape[0]
        top, ff = expert.shape[-1], sg.shape[1]
        slots = 5 * tokens * top // (4 * wg.shape[0] * mesh.shape["ep"])
        me, part = lax.axis_index("ep"), lax.axis_index("dp")
        bf = 512
        blocks = ff // 2 // bf
        early, relay = 15, 10

        code = jnp.where(slot < slots, expert * slots + slot, -1)[0, 0]
        weight = gate[0, 0].astype(jnp.bfloat16).astype(jnp.float32)
        small = jnp.stack([code.astype(jnp.float32).T, weight.T])
        h, xs, smalls = gather_up(x, small, sg, su, blocks, early, relay, bf)
        smalls = jnp.concatenate([small[None], smalls])
        base = jnp.reshape(me * wg.shape[0] * slots, (1,)).astype(jnp.int32)
        mine = jnp.reshape(part, (1,)).astype(jnp.int32)
        codes, picked, used = plan_call(smalls, base, mine, slots)
        gates = smalls[:, 1]
        out = routed_call(x, xs, codes, picked, used, wg, wu, wd, slots, 512)

        y = reduce_up_down(x, xs, h, out, codes, gates, sg, su, sd, slots, bf)
        return y[None, None]

    lead = P("dp", "ep", None, None)
    return jax.shard_map(
        body,
        mesh=mesh,
        in_specs=(lead,) * 4 + (P("ep", None, None),) * 3 + (P(None, None),) * 3,
        out_specs=lead,
        check_vma=False,
    )
```

profile of v0, /device:TPU:0, one launch (start us, length us, event | category | flops | bytes accessed | tf_op | source)
XLA Modules:
  0.0 308.5 jit_solution(14460912571226035988)
XLA Ops:
  0.0 0.7 convert_bitcast_fusion.1
  0.7 0.7 convert_bitcast_fusion
  1.4 0.6 pad_maximum_fusion.1
  2.0 77.5 %gather_up.1 = (bf16[512,7680]{1,0:T(8,128)(2,1)}, bf16[7,256,3584]{2,1,0:T(8,128)(2,1)}, f32[7,2,8,256]{3,2,1,0:T(8,128)}) custom-call(bf16[256,3584]{1,0:T(8,128)(2,1)} %bitcast.21, f32[2,8,256]{2,1,0:T(8,128)} %get-tuple-element.17.small_ref, bf16[3584,20480]{1,0:T(8,128)(2,1)} %refs_5_.1, bf16[3584,20480]{1,0:T(8,128)(2,1)} %refs_6_.1), custom_call_target="tpu_custom_call" | custom-call | flops 56371445760 | bytes 110100480 | tf_op jit(solution)/shard_map/gather_up/pallas_call | solution.py:122
  79.6 1.4 fusion.1.refs_1_
  81.0 0.9 pad_maximum_fusion
  81.9 0.7 copy.12.small_ref
  82.6 2.0 plan.1
  84.6 124.0 %routed.1.refs_4_ = bf16[4,2,5,4,16,3584]{5,4,3,2,1,0:T(8,128)(2,1)} custom-call(s32[4]{0:T(128)} %get-tuple-element.14.picked_ref, s32[4,2]{1,0:T(4,128)} %get-tuple-element.15.used_ref, f32[8,8,256]{2,1,0:T(8,128)} %get-tuple-element.12.code_ref.refs_0_, bf16[256,3584]{1,0:T(8,128)(2,1)} %bitcast.22, ...), custom_call_target="tpu_custom_call" | custom-call | flops 93952409600 | bytes 220200960 | tf_op jit(solution)/shard_map/routed/pallas_call | solution.py:503
  208.6 97.0 %reduce_up_down.1 = bf16[256,3584]{1,0:T(8,128)(2,1)} custom-call(f32[8,8,256]{2,1,0:T(8,128)} %get-tuple-element.12.code_ref.refs_0_, f32[8,8,256]{2,1,0:T(8,128)} %fusion.1.refs_1_, bf16[256,3584]{1,0:T(8,128)(2,1)} %bitcast.23, bf16[7,256,3584]{2,1,0:T(8,128)(2,1)} %get-tuple-element.13.xs_ref.refs_3_, bf16[4,2,5,4,16,3584]{5,4,3,2,1,0:T(8,128)(2,1)} %routed.1.refs_4_, ...), custom_call_target="tpu_custom_call" | custom-call | flops 56371445760 | bytes 110100480 | tf_op jit(solution)/shard_map/reduce_up_down/pallas_call | solution.py:345
  305.6 2.8 copy.18
where the time goes:
time: 313 us; the launch traced here: 308 us
  Pallas kernels  301 us (96%)
  other arithmetic  4.37 us (1%)
  local copies, waits for them, and re-layouts  3.51 us (1%)
    pallas_call x1, Pallas kernels, routed_call(): pl.pallas_call(kern, out_shape=jax.ShapeDtypeStruct((experts, groups, chu...  124 us
    pallas_call x1, Pallas kernels, reduce_up_down(): pl.pallas_call(kern, out_shape=jax.ShapeDtypeStruct((half, d), bf16), gri...  97 us
    pallas_call x1, Pallas kernels, gather_up(): pl.pallas_call(kern, out_shape=[jax.ShapeDtypeStruct((2 * tokens, blocks...  77.5 us

commit v1 on v0

--- a/solution.py
+++ b/solution.py
@@ -98,15 +98,18 @@
             for c in second:
                 c.start()
 
-        @pl.when(i > 0)
-        def _():
-            h_ref[...] = up(x2[...])
-
         @pl.when(i == blocks - 1)
         def _():
             second[0].wait_recv()
             second[1].wait_recv()
             third[0].start()
+
+        @pl.when(i > 0)
+        def _():
+            h_ref[...] = up(x2[...])
+
+        @pl.when(i == blocks - 1)
+        def _():
             second[2].wait_recv()
             second[3].wait_recv()
             for c in little:
@@ -166,7 +169,7 @@
     mid0 = up0 + ups
     down0 = mid0 + 2
     steps = down0 + blocks
-    bn = 512
+    bn = 1792
     f32, bf16 = jnp.float32, jnp.bfloat16
 
     def kern(*refs):
@@ -383,14 +386,17 @@
     )(codes, gates, x, xs, out, sg, su, h, sd)
 
 
-def plan_call(smalls, base, part, slots):
-    n_src, _, top, tokens = smalls.shape
+def plan_call(small, smalls, base, part, slots):
+    n_src, top, tokens = 1 + smalls.shape[0], *smalls.shape[2:]
     groups = n_src // 4
     experts = 4 * groups
 
-    def kern(base_ref, part_ref, small_ref, code_ref, expert_ref, used_ref):
+    def kern(base_ref, part_ref, own_ref, small_ref, code_ref, gate_ref, expert_ref, used_ref):
         low = base_ref[0].astype(jnp.float32)
-        codes = [small_ref[s, 0] - low for s in range(n_src)]
+        codes = [own_ref[0] - low] + [small_ref[s, 0] - low for s in range(n_src - 1)]
+        gate_ref[0] = own_ref[1]
+        for s in range(1, n_src):
+            gate_ref[s] = small_ref[s - 1, 1]
         used, total = [], []
         for e in range(experts):
             counts = []
@@ -426,17 +432,18 @@
             code_ref[s] = news[s]
 
     smem = pl.BlockSpec(memory_space=pltpu.SMEM)
+    vmem = pl.BlockSpec(memory_space=pltpu.VMEM)
     return pl.pallas_call(
         kern,
-        out_shape=[
-            jax.ShapeDtypeStruct((n_src, top, tokens), jnp.float32),
+        out_shape=[jax.ShapeDtypeStruct((n_src, top, tokens), jnp.float32)] * 2
+        + [
             jax.ShapeDtypeStruct((experts // groups,), jnp.int32),
             jax.ShapeDtypeStruct((experts // groups, groups), jnp.int32),
         ],
-        in_specs=[smem, smem, pl.BlockSpec(memory_space=pltpu.VMEM)],
-        out_specs=[pl.BlockSpec(memory_space=pltpu.VMEM), smem, smem],
+        in_specs=[smem, smem, vmem, vmem],
+        out_specs=[vmem, vmem, smem, smem],
         name="plan",
-    )(base, part, smalls)
+    )(base, part, small, smalls)
 
 
 def routed_call(x, xs, codes, picked, used, wg, wu, wd, slots, bf):
@@ -543,19 +550,16 @@
         me, part = lax.axis_index("ep"), lax.axis_index("dp")
         bf = 512
         blocks = ff // 2 // bf
-        early, relay = 15, 10
+        early, relay = 16, 10
 
         code = jnp.where(slot < slots, expert * slots + slot, -1)[0, 0]
         weight = gate[0, 0].astype(jnp.bfloat16).astype(jnp.float32)
         small = jnp.stack([code.astype(jnp.float32).T, weight.T])
         h, xs, smalls = gather_up(x, small, sg, su, blocks, early, relay, bf)
-        smalls = jnp.concatenate([small[None], smalls])
         base = jnp.reshape(me * wg.shape[0] * slots, (1,)).astype(jnp.int32)
         mine = jnp.reshape(part, (1,)).astype(jnp.int32)
-        codes, picked, used = plan_call(smalls, base, mine, slots)
-        gates = smalls[:, 1]
+        codes, gates, picked, used = plan_call(small, smalls, base, mine, slots)
         out = routed_call(x, xs, codes, picked, used, wg, wu, wd, slots, 512)
-
         y = reduce_up_down(x, xs, h, out, codes, gates, sg, su, sd, slots, bf)
         return y[None, None]
 

time: 313 us -> 306 us (0.978)
  Pallas kernels: 301 us -> 297 us
    pallas_call x1, Pallas kernels: 124 us -> 112 us  [routed_call(): pl.pallas_call(kern, out_shape=jax.ShapeDtypeStruct((experts, groups, chu...]
    pallas_call x1, Pallas kernels: 97 us -> 105 us  [reduce_up_down(): pl.pallas_call(kern, out_shape=jax.ShapeDtypeStruct((half, d), bf16), gri...]
where the time goes in v1:
time: 306 us; the launch traced here: 302 us
  Pallas kernels  297 us (97%)
    pallas_call x1, Pallas kernels, routed_call(): pl.pallas_call(kern, out_shape=jax.ShapeDtypeStruct((experts, groups, chu...  112 us
    pallas_call x1, Pallas kernels, reduce_up_down(): pl.pallas_call(kern, out_shape=jax.ShapeDtypeStruct((half, d), bf16), gri...  105 us
    pallas_call x1, Pallas kernels, gather_up(): pl.pallas_call(kern, out_shape=[jax.ShapeDtypeStruct((2 * tokens, blocks...  78.2 us

profile of v1, /device:TPU:0, one launch (start us, length us, event | category | flops | bytes accessed | tf_op | source)
XLA Modules:
  0.0 302.4 jit_solution(17566419750716866545)
XLA Ops:
  0.0 0.7 convert_bitcast_fusion.1
  0.7 0.7 convert_bitcast_fusion
  1.4 0.6 pad_maximum_fusion.small_ref.own_ref
  2.0 78.2 %gather_up.1 = (bf16[512,8192]{1,0:T(8,128)(2,1)}, bf16[7,256,3584]{2,1,0:T(8,128)(2,1)}, f32[7,2,8,256]{3,2,1,0:T(8,128)}) custom-call(bf16[256,3584]{1,0:T(8,128)(2,1)} %bitcast.17, f32[2,8,256]{2,1,0:T(8,128)} %pad_maximum_fusion.small_ref.own_ref, bf16[3584,20480]{1,0:T(8,128)(2,1)} %refs_5_.1, bf16[3584,20480]{1,0:T(8,128)(2,1)} %refs_6_.1), custom_call_target="tpu_custom_call" | custom-call | flops 60129542144 | bytes 117440512 | tf_op jit(solution)/shard_map/gather_up/pallas_call | solution.py:125
  80.2 2.0 plan.1
  82.2 112.0 %routed.1.refs_4_ = bf16[4,2,5,4,16,3584]{5,4,3,2,1,0:T(8,128)(2,1)} custom-call(s32[4]{0:T(128)} %get-tuple-element.16.picked_ref, s32[4,2]{1,0:T(4,128)} %get-tuple-element.17.used_ref, f32[8,8,256]{2,1,0:T(8,128)} %get-tuple-element.13.code_ref.refs_0_, bf16[256,3584]{1,0:T(8,128)(2,1)} %bitcast.18, ...), custom_call_target="tpu_custom_call" | custom-call | flops 93952409600 | bytes 220200960 | tf_op jit(solution)/shard_map/routed/pallas_call | solution.py:510
  194.2 105.3 %reduce_up_down.1 = bf16[256,3584]{1,0:T(8,128)(2,1)} custom-call(f32[8,8,256]{2,1,0:T(8,128)} %get-tuple-element.13.code_ref.refs_0_, f32[8,8,256]{2,1,0:T(8,128)} %get-tuple-element.14.refs_1_, bf16[256,3584]{1,0:T(8,128)(2,1)} %bitcast.19, bf16[7,256,3584]{2,1,0:T(8,128)(2,1)} %get-tuple-element.15.xs_ref.refs_3_, ...), custom_call_target="tpu_custom_call" | custom-call | flops 52613349376 | bytes 102760448 | tf_op jit(solution)/shard_map/reduce_up_down/pallas_call | solution.py:348
  299.5 2.8 copy.12
